TPU v7x, 256 devices: a whole 4x4x8 slice. The times are simulated.
256 devices in a mesh: ep: 8 (over y_lo, x), fsdp: 32 (over z, y_hi, core).
Axes of the slice: x: 4, y: 4 (y_hi: 2, y_lo: 2; y = y_hi * 2 + y_lo), z: 8, core: 2. Of those that a mesh axis runs over, the one named last changes fastest.
Arguments:
- train_gate: float32 [64, 2048, 1408], P('ep', 'fsdp'), may hold values from -0.25 to 0.25
- train_up: float32 [64, 2048, 1408], P('ep', 'fsdp'), may hold values from -0.25 to 0.25
- train_down: float32 [64, 1408, 2048], P('ep', None, 'fsdp'), may hold values from -0.3125 to 0.3125
- router_weight: float32 [2048, 64], P('fsdp', 'ep'), may hold values from -0.125 to 0.125
- router_gain: float32 [2048], P('fsdp'), may hold values from 0.25 to 1.75
Outputs:
- ready_gate: bfloat16 [64, 2048, 1408], P('ep', None, 'fsdp')
- ready_up: bfloat16 [64, 2048, 1408], P('ep', None, 'fsdp')
- ready_down: bfloat16 [64, 1408, 2048], P('ep', 'fsdp')
- scale_gate: float32 [64, 1408], P('ep', 'fsdp')
- scale_up: float32 [64, 1408], P('ep', 'fsdp')
- scale_down: float32 [64, 1408], P('ep', 'fsdp')
- serve_router: bfloat16 [2048, 64], replicated
All inputs are finite; a program needn't handle non-finite values. Where the computation divides by a largest or mean magnitude, that divisor is 1e-20 or more.
Results may differ from a plain program's by a relative error of at most 0.001.
Values may be sent and summed in bfloat16 or wider, within the bound.
A program may use at most 128 MiB of HBM per device.

v0:
```python
import jax
import jax.numpy as jnp
from jax import lax
from jax.sharding import PartitionSpec as P


def side_by_side(arrays, axis, split_dim, concat_dim, along):
    both = jnp.concatenate(arrays, axis=along)
    out, at, gathered = (
        lax.all_to_all(both, axis, split_axis=split_dim, concat_axis=concat_dim, tiled=True),
        0,
        [],
    )
    for a in arrays:
        gathered.append(lax.slice_in_dim(out, at, at + a.shape[along], axis=along))
        at += a.shape[along]
    return tuple(gathered)


def copy_for_each(x, axis):
    count = lax.axis_size(axis)
    return lax.all_to_all(jnp.broadcast_to(x[None], (count, *x.shape)), axis, 0, 0, tiled=True)


def laid_out(tiles, dim):
    shape = list(tiles.shape[1:])
    shape[dim] *= tiles.shape[0]
    return jnp.moveaxis(tiles, 0, dim).reshape(shape)


def gather_directly(x, axis, dim):
    tiles = copy_for_each(x, axis)
    return laid_out(tiles, dim)


def per_device(train_gate, train_up, train_down, router_weight, router_gain):
    whole_gate, whole_up = side_by_side((train_gate, train_up), "fsdp", 2, 1, 0)
    whole_down = lax.all_to_all(train_down, "fsdp", split_axis=1, concat_axis=2, tiled=True)
    scale_gate = jnp.max(jnp.abs(whole_gate), axis=1)
    ready_gate = (whole_gate / jnp.expand_dims(scale_gate, 1)).astype(jnp.bfloat16)
    scale_up = jnp.max(jnp.abs(whole_up), axis=1)
    ready_up = (whole_up / jnp.expand_dims(scale_up, 1)).astype(jnp.bfloat16)
    scale_down = jnp.max(jnp.abs(whole_down), axis=2)
    ready_down = (whole_down / jnp.expand_dims(scale_down, 2)).astype(jnp.bfloat16)
    part_router = (router_weight * router_gain[:, None]).astype(jnp.bfloat16)
    row_router = gather_directly(part_router, "fsdp", 0)
    serve_router = lax.all_gather(row_router, "ep", axis=1, tiled=True)
    return (ready_gate, ready_up, ready_down, scale_gate, scale_up, scale_down, serve_router)


def solution(mesh):
    placed = (
        P("ep", "fsdp", None),
        P("ep", "fsdp", None),
        P("ep", None, "fsdp"),
        P("fsdp", "ep"),
        P("fsdp"),
    )
    return jax.shard_map(
        per_device,
        mesh=mesh,
        in_specs=placed,
        out_specs=(
            P("ep", None, "fsdp"),
            P("ep", None, "fsdp"),
            P("ep", "fsdp", None),
            P("ep", "fsdp"),
            P("ep", "fsdp"),
            P("ep", "fsdp"),
            P(),
        ),
        check_vma=False,
    )
```

profile of v0, /device:TPU:1, one launch (start us, length us, event | category | flops | bytes accessed | tf_op | source)
XLA Modules:
  0.0 305.1 jit_solution(9510123068798029468)
XLA Ops:
  0.6 0.7 multiply_convert_fusion
  1.3 0.7 reshape.29
  2.1 12.7 %all-to-all-start.2 = ((bf16[32,2,256]{2,1,0:T(2,128)(2,1)}), bf16[32,2,256]{2,1,0:T(2,128)(2,1)S(1)}, u32[]{:S(2)}, u32[]{:S(2)}) async-start(bf16[32,2,256]{2,1,0:T(2,128)(2,1)} %reshape.29), calls=%async_computation.2 | async-start | bytes 65536 | tf_op jit(solution)/shard_map/all_to_all | solution.py:22
  14.8 5.4 %copy.45 = f32[8,1408,64]{2,0,1:T(8,128)} copy(f32[8,1408,64]{1,2,0:T(8,128)} %param.7) | data formatting | bytes 5767168 | tf_op args[2]
  20.2 6.7 %reshape.27 = f32[32,1,22528]{2,1,0:T(1,128)} reshape(f32[1408,8,64]{2,1,0:T(8,128)} %bitcast.31) | data formatting | bytes 5767168
  26.9 0.0 all-to-all-done.2
  27.0 9.8 %all-to-all-start.1 = ((f32[32,1,22528]{2,1,0:T(1,128)}), f32[32,1,22528]{2,1,0:T(1,128)S(1)}, u32[]{:S(2)}, u32[]{:S(2)}) async-start(f32[32,1,22528]{2,1,0:T(1,128)} %reshape.27), calls=%async_computation.1 | async-start | bytes 5767168 | tf_op jit(solution)/shard_map/all_to_all | solution.py:38
  36.7 5.4 %copy.41 = f32[8,64,1408]{1,0,2:T(8,128)} copy(f32[8,64,1408]{2,1,0:T(8,128)} %param.5) | data formatting | bytes 5767168 | tf_op args[0]
  42.1 5.4 %copy.42 = f32[8,64,1408]{1,0,2:T(8,128)} copy(f32[8,64,1408]{2,1,0:T(8,128)} %param.6) | data formatting | bytes 5767168 | tf_op args[1]
  47.5 9.7 %fusion = f32[1408,16,64]{2,1,0:T(8,128)} fusion(f32[8,64,1408]{1,0,2:T(8,128)} %copy.42, f32[8,64,1408]{1,0,2:T(8,128)} %copy.41), kind=kLoop, calls=%fused_computation.8 | loop fusion | flops 1441792 | bytes 11534336
  57.2 15.2 %reshape.25 = f32[32,1,45056]{2,1,0:T(1,128)} reshape(f32[1408,16,64]{2,1,0:T(8,128)} %fusion) | data formatting | bytes 11534336
  72.4 30.7 %all-to-all-done.1 = f32[32,1,22528]{2,1,0:T(1,128)S(1)} async-done(((f32[32,1,22528]{2,1,0:T(1,128)}), f32[32,1,22528]{2,1,0:T(1,128)S(1)}, u32[]{:S(2)}, u32[]{:S(2)}) %all-to-all-start.1) | async-done | bytes 2883616 | tf_op jit(solution)/shard_map/all_to_all | solution.py:38
  103.1 7.0 %all-to-all-start = ((f32[32,1,45056]{2,1,0:T(1,128)}), f32[32,1,45056]{2,1,0:T(1,128)}, u32[]{:S(2)}, u32[]{:S(2)}) async-start(f32[32,1,45056]{2,1,0:T(1,128)} %reshape.25), calls=%async_computation | async-start | bytes 11534336 | tf_op jit(solution)/shard_map/all_to_all | solution.py:10
  110.1 0.1 reshape.30
  110.2 0.1 reshape.24
  110.4 24.7 %all_gather.3 = bf16[2048,64]{0,1:T(8,128)(2,1)S(1)} all-gather(bf16[2048,8]{0,1:T(8,128)(2,1)S(1)} %reshape.24), channel_id=1, replica_groups=mesh['ep'=8,'fsdp'=32] {'ep'}, dimensions={1}, use_global_device_ids=true | all-gather | bytes 294912 | tf_op jit(solution)/shard_map/all_gather | solution.py:47
  135.1 0.5 broadcast.5
  135.6 9.9 %reduce.4 = f32[32,22528]{1,0:T(8,128)} reduce(f32[32,1,22528]{2,1,0:T(1,128)S(1)} %all-to-all-done.1, f32[]{:T(128)} %broadcast.5), dimensions={1}, to_apply=%all_to_all.30.reduce_sub_computation | reduce | bytes 5767172 | tf_op jit(solution)/shard_map/all_to_all | solution.py:38
  145.5 5.8 %reshape.28 = f32[1408,8,64]{2,1,0:T(8,128)} reshape(f32[32,22528]{1,0:T(8,128)} %reduce.4) | data formatting | bytes 5767168
  151.2 8.5 %copy.46 = f32[8,44,32,64]{3,2,0,1:T(8,128)} copy(f32[8,44,32,64]{3,0,1,2:T(8,128)} %bitcast.28) | data formatting | bytes 5767168 | tf_op jit(solution)/shard_map/all_to_all | solution.py:38
  159.7 4.2 %all_to_all.33 = f32[8,44,2048]{2,0,1:T(8,128)S(1)} reshape(f32[8,44,32,64]{3,2,0,1:T(8,128)} %copy.46) | data formatting | bytes 5767168 | tf_op jit(solution)/shard_map/all_to_all | solution.py:38
  164.0 3.3 %abs_reduce_fusion = f32[8,44]{0,1:T(8,128)S(1)} fusion(f32[8,44,32,64]{3,0,1,2:T(8,128)} %bitcast.29), kind=kLoop, calls=%fused_computation.1 | loop fusion | flops 1441440 | bytes 2884992 | tf_op jit(solution)/shard_map/reduce_max | solution.py:43
  167.3 0.7 copy.50
  167.9 1.5 divide_convert_fusion
  169.4 68.5 %all-to-all-done = f32[32,1,45056]{2,1,0:T(1,128)} async-done(((f32[32,1,45056]{2,1,0:T(1,128)}), f32[32,1,45056]{2,1,0:T(1,128)}, u32[]{:S(2)}, u32[]{:S(2)}) %all-to-all-start) | async-done | bytes 5767200 | tf_op jit(solution)/shard_map/all_to_all | solution.py:10
  238.0 18.8 %reduce.3 = f32[32,45056]{1,0:T(8,128)} reduce(f32[32,1,45056]{2,1,0:T(1,128)} %all-to-all-done, f32[]{:T(128)} %broadcast.5), dimensions={1}, to_apply=%all_to_all.27.reduce_sub_computation | reduce | bytes 11534340 | tf_op jit(solution)/shard_map/all_to_all | solution.py:10
  256.7 9.3 %reshape.26 = f32[1408,16,64]{2,1,0:T(8,128)} reshape(f32[32,45056]{1,0:T(8,128)} %reduce.3) | data formatting | bytes 11534336
  266.0 8.7 %abs_reduce_fusion.1 = (f32[8,44]{0,1:T(8,128)S(1)}, f32[8,44]{0,1:T(8,128)S(1)}, f32[8,32,64,44]{2,0,3,1:T(8,128)}, f32[8,32,64,44]{2,0,3,1:T(8,128)S(1)}) fusion(f32[16,32,64,44]{2,0,3,1:T(8,128)} %bitcast.30), kind=kLoop, calls=%fused_computation.2 | loop fusion | flops 2882880 | bytes 11537152 | tf_op jit(solution)/shard_map/reduce_max | solution.py:41
  274.7 5.8 %copy.43 = f32[8,32,64,44]{2,1,0,3:T(8,128)} copy(f32[8,32,64,44]{2,0,3,1:T(8,128)S(1)} %get-tuple-element.24) | data formatting | bytes 5767168 | tf_op jit(solution)/shard_map/slice | solution.py:15
  280.5 4.2 %slice.13 = f32[8,2048,44]{1,0,2:T(8,128)S(1)} reshape(f32[8,32,64,44]{2,1,0,3:T(8,128)} %copy.43) | data formatting | bytes 5767168 | tf_op jit(solution)/shard_map/slice | solution.py:15
  284.8 8.5 %copy.44 = f32[8,32,64,44]{2,1,0,3:T(8,128)} copy(f32[8,32,64,44]{2,0,3,1:T(8,128)} %get-tuple-element.23) | data formatting | bytes 5767168 | tf_op jit(solution)/shard_map/slice | solution.py:15
  293.2 5.6 %slice.15 = f32[8,2048,44]{1,0,2:T(8,128)} reshape(f32[8,32,64,44]{2,1,0,3:T(8,128)} %copy.44) | data formatting | bytes 5767168 | tf_op jit(solution)/shard_map/slice | solution.py:15
  298.8 0.7 copy.48
  299.5 0.7 copy.49
  300.2 4.2 %divide_convert_fusion.1 = (bf16[8,2048,44]{1,0,2:T(8,128)(2,1)}, bf16[8,2048,44]{1,0,2:T(8,128)(2,1)}) fusion(f32[8,2048,44]{1,0,2:T(8,128)} %slice.15, f32[8,44]{0,1:T(8,128)S(1)} %get-tuple-element.21, f32[8,2048,44]{1,0,2:T(8,128)S(1)} %slice.13, f32[8,44]{0,1:T(8,128)S(1)} %get-tuple-element.22), kind=kLoop, calls=%fused_computation.5 | loop fusion | flops 2883584 | bytes 8653568 | tf_op jit(solution)/shard_map/convert_element_type | solution.py:42
  304.4 0.7 copy.52
  (2 shorter events, 0.0 us)
Async XLA Ops:
  2.1 24.9 %all-to-all-start.2 = ((bf16[32,2,256]{2,1,0:T(2,128)(2,1)}), bf16[32,2,256]{2,1,0:T(2,128)(2,1)S(1)}, u32[]{:S(2)}, u32[]{:S(2)}) async-start(bf16[32,2,256]{2,1,0:T(2,128)(2,1)} %reshape.29), calls=%async_computation.2 | async-start | bytes 65536 | tf_op jit(solution)/shard_map/all_to_all | solution.py:22
  27.0 76.2 %all-to-all-start.1 = ((f32[32,1,22528]{2,1,0:T(1,128)}), f32[32,1,22528]{2,1,0:T(1,128)S(1)}, u32[]{:S(2)}, u32[]{:S(2)}) async-start(f32[32,1,22528]{2,1,0:T(1,128)} %reshape.27), calls=%async_computation.1 | async-start | bytes 5767168 | tf_op jit(solution)/shard_map/all_to_all | solution.py:38
  103.1 134.8 %all-to-all-start = ((f32[32,1,45056]{2,1,0:T(1,128)}), f32[32,1,45056]{2,1,0:T(1,128)}, u32[]{:S(2)}, u32[]{:S(2)}) async-start(f32[32,1,45056]{2,1,0:T(1,128)} %reshape.25), calls=%async_computation | async-start | bytes 11534336 | tf_op jit(solution)/shard_map/all_to_all | solution.py:10
where the time goes:
time: 309 us; the launch traced here: 305 us
  waiting for transfers between devices  99.2 us (32%)
  local copies, waits for them, and re-layouts  94.2 us (30%)
  other arithmetic  56.7 us (18%)
  starting transfers between devices  29.5 us (10%)
  blocking collectives  24.7 us (8%)
    all_to_all x1, waiting for transfers between devices, side_by_side(): lax.all_to_all(both, axis, split_axis=split_dim, concat_axis=concat_dim,...  68.5 us
    unnamed x14, local copies, waits for them, and re-layouts  56.7 us
    all_to_all x1, waiting for transfers between devices, per_device(): lax.all_to_all(train_down, 'fsdp', split_axis=1, concat_axis=2, tiled=True)  30.7 us
    all_gather x1, blocking collectives, per_device(): serve_router = lax.all_gather(row_router, 'ep', axis=1, tiled=True)  24.7 us
    slice x4, local copies, waits for them, and re-layouts, side_by_side(): gathered.append(lax.slice_in_dim(out, at, at + a.shape[along], axis=along))  24.1 us
    all_to_all x1, other arithmetic, side_by_side(): lax.all_to_all(both, axis, split_axis=split_dim, concat_axis=concat_dim,...  18.8 us
    all_to_all x1, starting transfers between devices, copy_for_each(): lax.all_to_all(jnp.broadcast_to(x[None], (count, *x.shape)), axis, 0, 0,...  12.7 us
    all_to_all x2, local copies, waits for them, and re-layouts, per_device(): lax.all_to_all(train_down, 'fsdp', split_axis=1, concat_axis=2, tiled=True)  12.7 us
  transfers between devices with their start and end apart: 3, of which 2 were waited for; matrix products, arithmetic and copies ran while one was open for 26% of the time, Pallas kernels for 0%

commit v1 on v0

v1 whole, which is shorter than its diff:
```python
import jax
import jax.numpy as jnp
from jax import lax
from jax.experimental import pallas as pl
from jax.experimental.pallas import tpu as pltpu
from jax.sharding import PartitionSpec as P

MESH = pl.DeviceIdType.MESH
N = 32
EP = 8
E, D, J = 8, 64, 1408
JT = J // 128
JD = J // N
ROWS = JD * E // 2
GROUPS = 4
PIECE = 384


def exchange(
    gate, up, down, rw, rg, land, scales, router,
    x, stage, sent, own_max, got_max, own_scale, all_scale, recip, rhalf, rtile,
    load_sem, rsend, rrecv, asend, arecv, dsend, drecv, dself,
    csend, crecv, zsend, zrecv, ysend, yrecv, esend, erecv, eself, out_sem,
):
    me = lax.axis_index("fsdp")
    ep = lax.axis_index("ep")
    z, yh, core = me // 4, lax.rem(me // 2, 2), lax.rem(me, 2)

    loads = []
    for m, ref in enumerate((gate, up, down)):
        loads.append(pltpu.make_async_copy(ref, x.at[m], load_sem.at[m]))
        loads[m].start()

    barrier = pltpu.get_barrier_semaphore()

    def greet(d, _):
        pl.semaphore_signal(barrier, inc=1, device_id={"fsdp": lax.rem(me + d, N)}, device_id_type=MESH)
        return 0

    def greet_ep(d, _):
        pl.semaphore_signal(barrier, inc=1, device_id={"ep": lax.rem(ep + d, EP)}, device_id_type=MESH)
        return 0

    lax.fori_loop(1, N, greet, 0)
    lax.fori_loop(1, EP, greet_ep, 0)

    part = rw[...] * rg[...]
    rhalf[0] = jnp.concatenate([part, part], axis=1)

    def maxima(m):
        def one(e, _):
            top = jnp.max(jnp.abs(x[m, e]), axis=0, keepdims=True)
            for g in range(GROUPS):
                w = min(PIECE, J - g * PIECE)
                own_max[m, e * GROUPS + g, :, :w] = top[:, g * PIECE : g * PIECE + w]
            return 0

        lax.fori_loop(0, E, one, 0)

    def send_maxima(m):
        def one(d, _):
            to = lax.rem(me + d, N)
            pltpu.make_async_remote_copy(
                own_max.at[m, to], got_max.at[m, me], rsend.at[m], rrecv.at[m], device_id={"fsdp": to}, device_id_type=MESH
            ).start()
            return 0

        lax.fori_loop(1, N, one, 0)

    def wait_bytes(ref, sem):
        pltpu.make_async_copy(ref, ref, sem).wait()

    def send_scales(m):
        got_max[m, me] = own_max[m, me]
        wait_bytes(got_max.at[m, pl.ds(0, N - 1)], rrecv.at[m])
        own_scale[m] = jnp.max(got_max[m], axis=0)
        all_scale[m, me] = own_scale[m]

        def one(d, _):
            to = lax.rem(me + d, N)
            pltpu.make_async_remote_copy(
                own_scale.at[m], all_scale.at[m, me], asend.at[m], arecv.at[m], device_id={"fsdp": to}, device_id_type=MESH
            ).start()
            return 0

        lax.fori_loop(1, N, one, 0)

    def send_matrix(m):
        wait_bytes(all_scale.at[m, pl.ds(0, N - 1)], arecv.at[m])
        for e in range(E):
            for g in range(GROUPS):
                recip[e : e + 1, g * PIECE : (g + 1) * PIECE] = 1.0 / all_scale[m, e * GROUPS + g]

        def tile(q, _):
            at = pl.multiple_of(q * 128, 128)
            for r in range(E // 2):
                v = x[m, 2 * r : 2 * r + 2, :, pl.ds(at, 128)] * recip[2 * r : 2 * r + 2, pl.ds(at, 128)][:, None, :]
                stage[pl.ds(r, 128, stride=E // 2), :] = v.reshape(128, 128).T
            sent[m, pl.ds(pl.multiple_of(q * 512, 512), 512), :] = stage[...].astype(jnp.bfloat16)
            return 0

        lax.fori_loop(0, JT, tile, 0)

        def rows_of(to):
            return sent.at[m, pl.ds(pl.multiple_of(to * ROWS, ROWS), ROWS)]

        def one(d, _):
            to = lax.rem(me + d, N)
            pltpu.make_async_remote_copy(
                rows_of(to), land.at[m, me], dsend.at[m], drecv.at[m], device_id={"fsdp": to}, device_id_type=MESH
            ).start()
            return 0

        lax.fori_loop(1, N, one, 0)
        pltpu.make_async_copy(rows_of(me), land.at[m, me], dself.at[m]).start()

    loads[0].wait()
    maxima(0)
    pl.semaphore_wait(barrier, N - 1 + EP - 1)
    send_maxima(0)
    router_core = pltpu.make_async_remote_copy(
        rhalf.at[0], rhalf.at[1], csend, crecv, device_id={"fsdp": me + 1 - 2 * core}, device_id_type=MESH
    )
    router_core.start()
    loads[1].wait()
    maxima(1)
    send_maxima(1)
    loads[2].wait()
    maxima(2)
    send_maxima(2)

    router_core.wait()
    lane = lax.broadcasted_iota(jnp.int32, (E, 128), 1)
    own_side = (lane // 64) == core
    rtile[yh, z] = jnp.where(own_side, rhalf[0], rhalf[1]).astype(jnp.bfloat16)

    def router_z(d, _):
        pltpu.make_async_remote_copy(
            rtile.at[yh, z], rtile.at[yh, z], zsend, zrecv,
            device_id={"fsdp": lax.rem(me + 4 * d, N)}, device_id_type=MESH,
        ).start()
        return 0

    lax.fori_loop(1, 8, router_z, 0)

    send_scales(0)
    send_scales(1)
    send_scales(2)
    send_matrix(0)

    wait_bytes(rtile.at[0, pl.ds(0, 7)], zrecv)
    router_y = pltpu.make_async_remote_copy(
        rtile.at[yh], rtile.at[yh], ysend, yrecv, device_id={"fsdp": me + 2 - 4 * yh}, device_id_type=MESH
    )
    router_y.start()
    send_matrix(1)
    router_y.wait_recv()

    def router_ep(d, _):
        for half in range(2):
            pltpu.make_async_remote_copy(
                rtile.at[half], router.at[ep, :, half], esend, erecv,
                device_id={"ep": lax.rem(ep + d, EP)}, device_id_type=MESH,
            ).start()
        return 0

    lax.fori_loop(1, EP, router_ep, 0)
    for half in range(2):
        pltpu.make_async_copy(rtile.at[half], router.at[ep, :, half], eself.at[half]).start()
    send_matrix(2)

    keep = pltpu.make_async_copy(all_scale, scales, out_sem)
    keep.start()
    wait_bytes(rtile.at[0, pl.ds(0, 7)], zsend)
    router_y.wait_send()
    wait_bytes(router.at[pl.ds(0, EP - 1)], esend)
    wait_bytes(router.at[pl.ds(0, EP - 1)], erecv)
    for half in range(2):
        pltpu.make_async_copy(rtile.at[half], router.at[ep, :, half], eself.at[half]).wait()
    for m in range(3):
        wait_bytes(own_max.at[m, pl.ds(0, N - 1)], rsend.at[m])
        wait_bytes(all_scale.at[m, pl.ds(0, N - 1)], asend.at[m])
    keep.wait()
    for m in range(3):
        pltpu.make_async_copy(sent.at[m, pl.ds(0, ROWS)], land.at[m, me], dself.at[m]).wait()
        wait_bytes(sent.at[m, pl.ds(0, (N - 1) * ROWS)], dsend.at[m])
        wait_bytes(land.at[m, pl.ds(0, N - 1)], drecv.at[m])


def merge(land, gate, up, down, rows):
    low = lax.broadcasted_iota(jnp.int32, (16, 128), 1) < 64
    for m, out in enumerate((gate, up, down)):
        for c in range(N // 2):
            a = land[m, 2 * c].astype(jnp.float32)
            b = land[m, 2 * c + 1].astype(jnp.float32)
            rows[m, c, pl.ds(0, 16, stride=2), :] = jnp.where(low, a, pltpu.roll(b, 64, 1))
            rows[m, c, pl.ds(1, 16, stride=2), :] = jnp.where(low, pltpu.roll(a, 64, 1), b)
        for c in range(N // 2):
            out[:, :, c * 128 : (c + 1) * 128] = rows[m, c].astype(jnp.bfloat16).reshape(4, E, 128)


def per_device(train_gate, train_up, train_down, router_weight, router_gain):
    f32, bf16 = jnp.float32, jnp.bfloat16
    anywhere = pl.BlockSpec(memory_space=pl.ANY)
    vmem = pl.BlockSpec(memory_space=pltpu.VMEM)
    dma = pltpu.SemaphoreType.DMA
    land, scales, router = pl.pallas_call(
        exchange,
        out_shape=(
            jax.ShapeDtypeStruct((3, N, ROWS, 128), bf16),
            jax.ShapeDtypeStruct((3, N, 1, PIECE), f32),
            jax.ShapeDtypeStruct((EP, 8, 2, E, 128), bf16),
        ),
        in_specs=[anywhere] * 3 + [vmem] * 2,
        out_specs=(anywhere,) * 3,
        scratch_shapes=[
            pltpu.VMEM((3, E, D, J), f32),
            pltpu.VMEM((512, 128), f32),
            pltpu.VMEM((3, N * ROWS, 128), bf16),
            pltpu.VMEM((3, N, 1, PIECE), f32),
            pltpu.VMEM((3, N, 1, PIECE), f32),
            pltpu.VMEM((3, 1, PIECE), f32),
            pltpu.VMEM((3, N, 1, PIECE), f32),
            pltpu.VMEM((E, GROUPS * PIECE), f32),
            pltpu.VMEM((2, E, 128), f32),
            pltpu.VMEM((2, 8, E, 128), bf16),
        ]
        + [dma((3,))] * 8
        + [dma] * 8
        + [dma((2,)), dma],
        compiler_params=pltpu.CompilerParams(collective_id=0, has_side_effects=True, vmem_limit_bytes=60 * 2**20),
        name="exchange",
    )(
        train_gate,
        train_up,
        jnp.transpose(train_down, (0, 2, 1)),
        jnp.transpose(router_weight),
        router_gain[None, :],
    )
    ready = jax.ShapeDtypeStruct((JD, E, D * N), bf16)
    block = pl.BlockSpec((4, E, D * N), lambda i: (i, 0, 0))
    gate, up, down = pl.pallas_call(
        merge,
        grid=(JD // 4,),
        out_shape=(ready,) * 3,
        in_specs=[pl.BlockSpec((3, N, 16, 128), lambda i: (0, 0, i, 0))],
        out_specs=(block,) * 3,
        scratch_shapes=[pltpu.VMEM((3, N // 2, 32, 128), f32)],
        compiler_params=pltpu.CompilerParams(dimension_semantics=("arbitrary",)),
        name="merge",
    )(land)
    at = lax.axis_index("fsdp") * JD
    mine = lax.dynamic_slice_in_dim(scales.reshape(3, E, GROUPS * PIECE), at, JD, 2)
    serve = jnp.transpose(router, (0, 3, 1, 2, 4)).reshape(EP * E, D * N)
    return (
        jnp.transpose(gate, (1, 2, 0)),
        jnp.transpose(up, (1, 2, 0)),
        jnp.transpose(down, (1, 0, 2)),
        mine[0],
        mine[1],
        mine[2],
        jnp.transpose(serve),
    )


def solution(mesh):
    placed = (
        P("ep", "fsdp", None),
        P("ep", "fsdp", None),
        P("ep", None, "fsdp"),
        P("fsdp", "ep"),
        P("fsdp"),
    )
    return jax.shard_map(
        per_device,
        mesh=mesh,
        in_specs=placed,
        out_specs=(
            P("ep", None, "fsdp"),
            P("ep", None, "fsdp"),
            P("ep", "fsdp", None),
            P("ep", "fsdp"),
            P("ep", "fsdp"),
            P("ep", "fsdp"),
            P(),
        ),
        check_vma=False,
    )
```

time: 309 us -> 133 us (0.43); the launches traced: 305 us -> 133 us
  Pallas kernels: 0 us -> 129 us
  waiting for transfers between devices: 99.2 us -> 0 us
  local copies, waits for them, and re-layouts: 94.2 us -> 1.42 us
  other arithmetic: 56.7 us -> 1.3 us
  starting transfers between devices: 29.5 us -> 0 us
  blocking collectives: 24.7 us -> 0 us
    pallas_call x0 -> x2, Pallas kernels: none -> 129 us  [the longest x1 121 us: per_device(): pl.pallas_call(exchange, out_shape=(jax.ShapeDtypeStruct((3, N, ROWS, 128...]
    all_to_all x3 -> x0, waiting for transfers between devices: 99.2 us -> none  [the longest x1 68.5 us: side_by_side(): lax.all_to_all(both, axis, split_axis=split_dim, concat_axis=concat_dim,...]
    unnamed x14 -> x3, local copies, waits for them, and re-layouts: 56.7 us -> 0.71 us
    all_to_all x3 -> x0, starting transfers between devices: 29.5 us -> none  [the longest x1 12.7 us: copy_for_each(): lax.all_to_all(jnp.broadcast_to(x[None], (count, *x.shape)), axis, 0, 0,...]
    all_to_all x2 -> x0, other arithmetic: 28.6 us -> none  [the longest x1 18.8 us: side_by_side(): lax.all_to_all(both, axis, split_axis=split_dim, concat_axis=concat_dim,...]
    all_gather x1 -> x0, blocking collectives: 24.7 us -> none  [per_device(): serve_router = lax.all_gather(row_router, 'ep', axis=1, tiled=True)]
    slice x4 -> x0, local copies, waits for them, and re-layouts: 24.1 us -> none  [side_by_side(): gathered.append(lax.slice_in_dim(out, at, at + a.shape[along], axis=along))]
    all_to_all x4 -> x0, local copies, waits for them, and re-layouts: 13.2 us -> none  [the longest x2 12.7 us: per_device(): lax.all_to_all(train_down, 'fsdp', split_axis=1, concat_axis=2, tiled=True)]
  transfers between devices with their start and end apart: 3 -> 0, of which waited for: 2 -> 0; matrix products, arithmetic and copies ran while one was open for 26% -> 0% of each run, Pallas kernels for 0% -> 0%
where the time goes in v1:
time: 133 us
  Pallas kernels  129 us (97%)
  local copies, waits for them, and re-layouts  1.42 us (1%)
    pallas_call x1, Pallas kernels, per_device(): pl.pallas_call(exchange, out_shape=(jax.ShapeDtypeStruct((3, N, ROWS, 128...  121 us
    pallas_call x1, Pallas kernels, per_device(): pl.pallas_call(merge, grid=(JD // 4,), out_shape=(ready,) * 3, in_specs=[...  8.59 us

profile of v1, /device:TPU:1, one launch (start us, length us, event | category | flops | bytes accessed | tf_op | source)
XLA Modules:
  0.0 132.7 jit_solution(11517274769368911124)
XLA Ops:
  0.6 120.7 %exchange.1 = (bf16[3,32,176,128]{3,2,1,0:T(8,128)(2,1)}, f32[3,32,1,384]{3,2,1,0:T(1,128)}, bf16[8,8,2,8,128]{4,3,2,1,0:T(8,128)(2,1)}) custom-call(f32[8,64,1408]{2,1,0:T(8,128)} %gate.1, f32[8,64,1408]{2,1,0:T(8,128)} %up.1, f32[8,64,1408]{2,1,0:T(8,128)} %bitcast.17, f32[8,64]{1,0:T(8,128)} %bitcast.19, f32[1,64]{1,0:T(1,128)} %bitcast.20), custom_call_target="tpu_custom_call" | custom-call | tf_op jit(solution)/shard_map/exchange/pallas_call | solution.py:207
  121.4 0.0 copy-start
  121.4 1.3 reduce
  122.7 0.7 dynamic-slice_bitcast_fusion
  123.4 8.6 %merge.1 = (bf16[44,8,2048]{2,1,0:T(8,128)(2,1)}, bf16[44,8,2048]{2,1,0:T(8,128)(2,1)}, bf16[44,8,2048]{2,1,0:T(8,128)(2,1)}) custom-call(bf16[3,32,176,128]{3,2,1,0:T(8,128)(2,1)} %get-tuple-element.13.land), custom_call_target="tpu_custom_call" | custom-call | tf_op jit(solution)/shard_map/merge/pallas_call | solution.py:242
  132.0 0.0 copy-done
  132.0 0.7 copy.13
  (1 shorter events, 0.0 us)
Async XLA Ops:
  121.4 10.6 %copy-start = (bf16[8,8,2,8,128]{4,3,2,1,0:T(8,128)(2,1)S(1)}, bf16[8,8,2,8,128]{4,3,2,1,0:T(8,128)(2,1)}, u32[]{:S(2)}) copy-start(bf16[8,8,2,8,128]{4,3,2,1,0:T(8,128)(2,1)} %get-tuple-element.18) | copy-start | bytes 786436

commit v2 on v1

v2 whole, which is shorter than its diff:
```python
import jax
import jax.numpy as jnp
from jax import lax
from jax.experimental import pallas as pl
from jax.experimental.pallas import tpu as pltpu
from jax.sharding import PartitionSpec as P

MESH = pl.DeviceIdType.MESH
N = 32
EP = 8
E, D, J = 8, 64, 1408
JT = J // 128
JD = J // N
ROWS = JD * E // 2
CJ = 128 // E
LINES = -(-JD // CJ)
WIDE = J + 128
FAR_FIRST = (4, 3, 5, 2, 6, 1, 7, 0)
ARRIVAL = (0, 4, 3, 5, 2, 6, 1, 7)
EARLY = 4

LEVELS, STEPS, LOWEST = 30720, 128, 120


def encode(x, per_unit):
    n = jnp.floor(jnp.abs(x) * per_unit + 0.5)
    high = jnp.floor(n * (1 / STEPS))
    v = jnp.exp2(high - LOWEST) * (1.0 + (n - STEPS * high) * (1 / STEPS))
    return jnp.where(x < 0, -v, v)


def decode(v):
    size = jnp.abs(v)
    high = jnp.floor(jnp.log2(size))
    n = (high + (LOWEST - 1.0)) * STEPS + size * jnp.exp2(-high) * STEPS
    return jnp.where(v < 0, -n, n)


def exchange(
    gate, up, down, rw, rg, gate_out, up_out, down_out, scales, router,
    x, stage, sent, land, rows, tops, spread, recip, lines, got_lines, inv, fac, rw_v, rg_v, rhalf, rtile,
    load_sem, rload, lsend, lrecv, dsend, drecv, dself,
    csend, crecv, zsend, zrecv, ysend, yrecv, esend, erecv, eself,
):
    me = lax.axis_index("fsdp")
    ep = lax.axis_index("ep")
    z, yh, core = me // 4, lax.rem(me // 2, 2), lax.rem(me, 2)
    first = (JT * me) // N
    lane = lax.broadcasted_iota(jnp.int32, (E, 128), 1)
    row = lax.broadcasted_iota(jnp.int32, (E, 128), 0)

    loads = []
    for m, ref in enumerate((gate, up, down)):
        loads.append(pltpu.make_async_copy(ref, x.at[m], load_sem.at[m]))
        loads[m].start()
    rloads = [pltpu.make_async_copy(a, b, rload.at[i]) for i, (a, b) in enumerate(((rw, rw_v), (rg, rg_v)))]
    for load in rloads:
        load.start()

    barrier = pltpu.get_barrier_semaphore()

    def greet(d, _):
        pl.semaphore_signal(barrier, inc=1, device_id={"fsdp": lax.rem(me + d, N)}, device_id_type=MESH)
        return 0

    def greet_ep(d, _):
        pl.semaphore_signal(barrier, inc=1, device_id={"ep": lax.rem(ep + d, EP)}, device_id_type=MESH)
        return 0

    lax.fori_loop(1, N, greet, 0)
    lax.fori_loop(1, EP, greet_ep, 0)

    def wait_bytes(ref, sem):
        pltpu.make_async_copy(ref, ref, sem).wait()

    def maxima(m):
        def one(e, _):
            tops[m, pl.ds(e, 1), :J] = jnp.max(jnp.abs(x[m, e]), axis=0, keepdims=True)
            return 0

        tops[m, :, J:] = jnp.zeros((E, WIDE - J), jnp.float32)
        lax.fori_loop(0, E, one, 0)

    def scaling(m):
        top = tops[m]
        recip[...] = jnp.where(top > 1e-30, LEVELS / jnp.maximum(top, 1e-30), 0.0)

    def listed(values, i):
        found = 0
        for at, value in enumerate(values):
            found = jnp.where(i == at, value, found)
        return found

    def lay_out(m, i):
        q = lax.rem(first + i, JT)
        at = pl.multiple_of(q * 128, 128)
        for r in range(E // 2):
            v = encode(x[m, 2 * r : 2 * r + 2, :, pl.ds(at, 128)], recip[2 * r : 2 * r + 2, pl.ds(at, 128)][:, None, :])
            stage[pl.ds(r, 128, stride=E // 2), :] = v.reshape(128, 128).T
        sent[m, pl.ds(pl.multiple_of(q * 512, 512), 512), :] = stage[...].astype(jnp.bfloat16)

    def rows_of(m, to):
        return sent.at[m, pl.ds(pl.multiple_of(to * ROWS, ROWS), ROWS)]

    def send_rows(m, to):
        @pl.when(to != me)
        def _():
            pltpu.make_async_remote_copy(
                rows_of(m, to), land.at[m, me], dsend.at[m], drecv.at[m, me], device_id={"fsdp": to}, device_id_type=MESH
            ).start()

        @pl.when(to == me)
        def _():
            pltpu.make_async_copy(rows_of(m, to), land.at[m, me], dself.at[m]).start()

    def send_tile(m, i):
        q = lax.rem(first + i, JT)
        to = (N * q) // JT

        @pl.when(jnp.logical_or(i > 0, (JT * to) // N >= q))
        def _():
            send_rows(m, to)

        for more in (1, 2):

            @pl.when(to + more < (N * (q + 1)) // JT)
            def _():
                send_rows(m, to + more)

    def tiles(m, start, stop, make=True, send=True):
        def one(i, _):
            if make:
                lay_out(m, i)
            if send:
                send_tile(m, i)
            return 0

        lax.fori_loop(start, stop, one, 0)

    def send_last(m):
        to = (N * first) // JT

        @pl.when((JT * to) // N < first)
        def _():
            send_rows(m, to)

    def send_far_first(m):
        lax.fori_loop(0, JT, lambda i, _: (lay_out(m, i), 0)[1], 0)

        def one(i, _):
            to = 4 * lax.rem(z + listed(FAR_FIRST, i // 4), 8) + lax.rem(me + i, 4)
            send_rows(m, to)
            return 0

        lax.fori_loop(0, N, one, 0)

    own_lanes = (lane // CJ) == row

    def draw_lines(m):
        for e in range(E):
            spread[e : e + 1, :] = pltpu.roll(tops[m, e : e + 1], CJ * e, 1)

        def one(to, _):
            for g in range(LINES):
                c0 = JD * to + CJ * g
                at = pl.multiple_of((c0 // 128) * 128, 128)
                near = pltpu.roll(spread[:, pl.ds(at, 256)], 256 - lax.rem(c0, 128), 1)[:, :128]
                g0 = (LINES * m + g) * 128
                lines[to, :, g0 : g0 + 128] = jnp.sum(jnp.where(own_lanes, near, 0.0), axis=0, keepdims=True)
            return 0

        lax.fori_loop(0, N, one, 0)

    loads[0].wait()
    maxima(0)
    scaling(0)
    tiles(0, 0, EARLY, send=False)
    pl.semaphore_wait(barrier, N - 1 + EP - 1)
    tiles(0, 0, EARLY, make=False)
    tiles(0, EARLY, JT)
    send_last(0)

    for load in rloads:
        load.wait()
    part = rw_v[...] * rg_v[...]
    rhalf[0] = jnp.concatenate([part, part], axis=1)
    router_core = pltpu.make_async_remote_copy(
        rhalf.at[0], rhalf.at[1], csend, crecv, device_id={"fsdp": me + 1 - 2 * core}, device_id_type=MESH
    )
    router_core.start()
    loads[1].wait()
    loads[2].wait()
    maxima(1)
    maxima(2)
    draw_lines(0)
    draw_lines(1)
    draw_lines(2)
    got_lines[me] = lines[me]

    def send_line(d, _):
        to = lax.rem(me + d, N)
        pltpu.make_async_remote_copy(
            lines.at[to], got_lines.at[me], lsend, lrecv, device_id={"fsdp": to}, device_id_type=MESH
        ).start()
        return 0

    lax.fori_loop(1, N, send_line, 0)

    router_core.wait()
    own_side = (lane // 64) == core
    rtile[yh, z] = jnp.where(own_side, rhalf[0], rhalf[1]).astype(jnp.bfloat16)

    def router_z(d, _):
        pltpu.make_async_remote_copy(
            rtile.at[yh, z], rtile.at[yh, z], zsend, zrecv,
            device_id={"fsdp": lax.rem(me + 4 * d, N)}, device_id_type=MESH,
        ).start()
        return 0

    lax.fori_loop(1, 8, router_z, 0)

    scaling(1)
    send_far_first(1)

    scaling(2)
    send_far_first(2)
    wait_bytes(rtile.at[0, pl.ds(0, 7)], zrecv)
    router_y = pltpu.make_async_remote_copy(
        rtile.at[yh], rtile.at[yh], ysend, yrecv, device_id={"fsdp": me + 2 - 4 * yh}, device_id_type=MESH
    )
    router_y.start()
    wait_bytes(got_lines.at[pl.ds(0, N - 1)], lrecv)
    router_y.wait_recv()

    def router_ep(d, _):
        for half in range(2):
            pltpu.make_async_remote_copy(
                rtile.at[half], router.at[ep, :, half], esend, erecv,
                device_id={"ep": lax.rem(ep + d, EP)}, device_id_type=MESH,
            ).start()
        return 0

    lax.fori_loop(1, EP, router_ep, 0)
    for half in range(2):
        pltpu.make_async_copy(rtile.at[half], router.at[ep, :, half], eself.at[half]).start()

    def side_by_side(a, b):
        low = lax.broadcasted_iota(jnp.int32, (ROWS, 128), 1) < 64
        rows[pl.ds(0, ROWS, stride=2), :] = jnp.where(low, a, pltpu.roll(b, 64, 1))
        rows[pl.ds(1, ROWS, stride=2), :] = jnp.where(low, pltpu.roll(a, 64, 1), b)
        return rows[...]

    def by_expert(line):
        line = jnp.broadcast_to(line, (E, 128))
        for_each = line
        for e in range(1, E):
            for_each = jnp.where(row == e, pltpu.roll(line, 128 - CJ * e, 1), for_each)
        return for_each

    def line_at(m, g):
        return pl.ds((LINES * m + g) * 128, 128)

    def merge(m, out):
        scale = jnp.zeros((E, 128), jnp.float32)
        for g in range(LINES):
            part = by_expert(jnp.max(got_lines[:, :, line_at(m, g)], axis=0))
            inv[g] = (1 / LEVELS) / jnp.where(part > 0, part, 1.0)
            scale = jnp.where(lane // CJ == g, pltpu.roll(part, CJ * g, 1), scale)
        scales[m] = scale
        pltpu.make_async_copy(rows_of(m, me), land.at[m, me], dself.at[m]).wait()
        low = lane < 64

        def chip(i, _):
            c = 2 * lax.rem(z + listed(ARRIVAL, i // 2), 8) + lax.rem(yh + i, 2)
            for g in range(LINES):
                per = [
                    by_expert(got_lines[2 * c + side, :, line_at(m, g)]) * inv[g] for side in range(2)
                ]
                for j in range(min(CJ, JD - CJ * g)):
                    a, b = (jnp.broadcast_to(p[:, j : j + 1], (E, 128)) for p in per)
                    fac[(CJ * g + j) * E : (CJ * g + j + 1) * E, :] = jnp.where(low, a, b)
            for side in range(2):

                @pl.when(2 * c + side != me)
                def _():
                    wait_bytes(land.at[m, 2 * c + side], drecv.at[m, 2 * c + side])

            a, b = (decode(land[m, 2 * c + side].astype(jnp.float32)) for side in range(2))
            v = (side_by_side(a, b) * fac[...]).astype(jnp.bfloat16)
            out[:, :, pl.ds(pl.multiple_of(c * 128, 128), 128)] = v.reshape(JD, E, 128)
            return 0

        lax.fori_loop(0, N // 2, chip, 0)

    merge(0, gate_out)
    wait_bytes(rtile.at[0, pl.ds(0, 7)], zsend)
    router_y.wait_send()
    wait_bytes(router.at[pl.ds(0, EP - 1)], esend)
    wait_bytes(router.at[pl.ds(0, EP - 1)], erecv)
    for half in range(2):
        pltpu.make_async_copy(rtile.at[half], router.at[ep, :, half], eself.at[half]).wait()
    merge(1, up_out)
    merge(2, down_out)
    wait_bytes(lines.at[pl.ds(0, N - 1)], lsend)
    for m in range(3):
        wait_bytes(sent.at[m, pl.ds(0, (N - 1) * ROWS)], dsend.at[m])


def finish(gate, up, down, scales, router, gate_out, up_out, down_out, sg, su, sd, router_out, cut, sem):
    copies = [
        pltpu.make_async_copy(a, b, sem.at[i])
        for i, (a, b) in enumerate(((gate, gate_out), (up, up_out), (down, down_out), (router, router_out)))
    ]
    for copy in copies:
        copy.start()
    cut[...] = scales[:, :, :JD]
    small = [pltpu.make_async_copy(cut.at[m], out, sem.at[4 + m]) for m, out in enumerate((sg, su, sd))]
    for copy in small:
        copy.start()
    for copy in copies + small:
        copy.wait()


def per_device(train_gate, train_up, train_down, router_weight, router_gain):
    f32, bf16 = jnp.float32, jnp.bfloat16
    hbm = pl.BlockSpec(memory_space=pltpu.HBM)
    vmem = pl.BlockSpec(memory_space=pltpu.VMEM)
    dma = pltpu.SemaphoreType.DMA

    def stay(a):
        return pltpu.with_memory_space_constraint(a, pltpu.HBM)

    ready = jax.ShapeDtypeStruct((JD, E, D * N), bf16)
    gate, up, down, scales, router = pl.pallas_call(
        exchange,
        out_shape=(
            *(ready,) * 3,
            jax.ShapeDtypeStruct((3, E, 128), f32),
            jax.ShapeDtypeStruct((EP, 8, 2, E, 128), bf16),
        ),
        in_specs=[hbm] * 5,
        out_specs=(vmem,) * 5,
        scratch_shapes=[
            pltpu.VMEM((3, E, D, J), f32),
            pltpu.VMEM((512, 128), f32),
            pltpu.VMEM((3, N * ROWS, 128), bf16),
            pltpu.VMEM((3, N, ROWS, 128), bf16),
            pltpu.VMEM((JD * E, 128), f32),
            pltpu.VMEM((3, E, WIDE), f32),
            pltpu.VMEM((E, WIDE), f32),
            pltpu.VMEM((E, WIDE), f32),
            pltpu.VMEM((N, 1, 3 * LINES * 128), f32),
            pltpu.VMEM((N, 1, 3 * LINES * 128), f32),
            pltpu.VMEM((LINES, E, 128), f32),
            pltpu.VMEM((JD * E, 128), f32),
            pltpu.VMEM((E, D), f32),
            pltpu.VMEM((1, D), f32),
            pltpu.VMEM((2, E, 128), f32),
            pltpu.VMEM((2, 8, E, 128), bf16),
        ]
        + [dma((3,)), dma((2,))]
        + [dma] * 2
        + [dma((3,)), dma((3, N)), dma((3,))]
        + [dma] * 8
        + [dma((2,))],
        compiler_params=pltpu.CompilerParams(collective_id=0, has_side_effects=True, vmem_limit_bytes=40 * 2**20),
        name="exchange",
    )(
        stay(train_gate),
        stay(train_up),
        stay(jnp.transpose(train_down, (0, 2, 1))),
        stay(jnp.transpose(router_weight)),
        stay(router_gain[None, :]),
    )
    scale = jax.ShapeDtypeStruct((E, JD), f32)
    gate, up, down, scale_gate, scale_up, scale_down, router = pl.pallas_call(
        finish,
        out_shape=(*(ready,) * 3, *(scale,) * 3, jax.ShapeDtypeStruct((EP, 8, 2, E, 128), bf16)),
        in_specs=[vmem] * 5,
        out_specs=(hbm,) * 7,
        scratch_shapes=[pltpu.VMEM((3, E, JD), f32), dma((7,))],
        compiler_params=pltpu.CompilerParams(vmem_limit_bytes=16 * 2**20),
        name="finish",
    )(gate, up, down, scales, router)
    serve = jnp.transpose(router, (0, 3, 1, 2, 4)).reshape(EP * E, D * N)
    return (
        jnp.transpose(gate, (1, 2, 0)),
        jnp.transpose(up, (1, 2, 0)),
        jnp.transpose(down, (1, 0, 2)),
        scale_gate,
        scale_up,
        scale_down,
        jnp.transpose(serve),
    )


def solution(mesh):
    placed = (
        P("ep", "fsdp", None),
        P("ep", "fsdp", None),
        P("ep", None, "fsdp"),
        P("fsdp", "ep"),
        P("fsdp"),
    )
    return jax.shard_map(
        per_device,
        mesh=mesh,
        in_specs=placed,
        out_specs=(
            P("ep", None, "fsdp"),
            P("ep", None, "fsdp"),
            P("ep", "fsdp", None),
            P("ep", "fsdp"),
            P("ep", "fsdp"),
            P("ep", "fsdp"),
            P(),
        ),
        check_vma=False,
    )
```

time: 133 us -> 116 us (0.87)
  Pallas kernels: 129 us -> 115 us
  local copies, waits for them, and re-layouts: 1.42 us -> 0 us
    pallas_call x2, Pallas kernels: 129 us -> 115 us  [the longest x1 113 us: per_device(): pl.pallas_call(exchange, out_shape=(*(ready,) * 3, jax.ShapeDtypeStruct((...]
where the time goes in v2:
time: 116 us
  Pallas kernels  115 us (99%)
    pallas_call x1, Pallas kernels, per_device(): pl.pallas_call(exchange, out_shape=(*(ready,) * 3, jax.ShapeDtypeStruct((...  113 us

profile of v2, /device:TPU:1, one launch (start us, length us, event | category | flops | bytes accessed | tf_op | source)
XLA Modules:
  0.0 116.0 jit_solution(11889813503579820544)
XLA Ops:
  0.6 113.2 %exchange.1 = (bf16[44,8,2048]{2,1,0:T(8,128)(2,1)S(1)}, bf16[44,8,2048]{2,1,0:T(8,128)(2,1)S(1)}, bf16[44,8,2048]{2,1,0:T(8,128)(2,1)S(1)}, f32[3,8,128]{2,1,0:T(8,128)S(1)}, bf16[8,8,2,8,128]{4,3,2,1,0:T(8,128)(2,1)S(1)}) custom-call(f32[8,64,1408]{2,1,0:T(8,128)} %gate.1, f32[8,64,1408]{2,1,0:T(8,128)} %up.1, f32[8,64,1408]{2,1,0:T(8,128)} %bitcast.11, ...), custom_call_target="tpu_custom_call" | custom-call | tf_op jit(solution)/shard_map/exchange/pallas_call | solution.py:334
  113.8 2.2 %finish.1 = (bf16[44,8,2048]{2,1,0:T(8,128)(2,1)}, bf16[44,8,2048]{2,1,0:T(8,128)(2,1)}, bf16[44,8,2048]{2,1,0:T(8,128)(2,1)}, f32[8,44]{1,0:T(8,128)}, f32[8,44...) custom-call(bf16[44,8,2048]{2,1,0:T(8,128)(2,1)S(1)} %get-tuple-element.19.gate, ...), custom_call_target="tpu_custom_call" | custom-call | tf_op jit(solution)/shard_map/finish/pallas_call | solution.py:376

commit v3 on v2

--- a/solution.py
+++ b/solution.py
@@ -17,7 +17,8 @@
 WIDE = J + 128
 FAR_FIRST = (4, 3, 5, 2, 6, 1, 7, 0)
 ARRIVAL = (0, 4, 3, 5, 2, 6, 1, 7)
-EARLY = 4
+TILES = (4, 7, 3, 8, 5, 6, 2, 9, 1, 10, 0)
+EARLY = 2
 
 LEVELS, STEPS, LOWEST = 30720, 128, 120
 
@@ -36,10 +37,17 @@
     return jnp.where(v < 0, -n, n)
 
 
+def listed(values, i):
+    found = 0
+    for at, value in enumerate(values):
+        found = jnp.where(i == at, value, found)
+    return found
+
+
 def exchange(
     gate, up, down, rw, rg, gate_out, up_out, down_out, scales, router,
     x, stage, sent, land, rows, tops, spread, recip, lines, got_lines, inv, fac, rw_v, rg_v, rhalf, rtile,
-    load_sem, rload, lsend, lrecv, dsend, drecv, dself,
+    tile_sem, load_sem, rload, lsend, lrecv, dsend, drecv, dself,
     csend, crecv, zsend, zrecv, ysend, yrecv, esend, erecv, eself,
 ):
     me = lax.axis_index("fsdp")
@@ -49,26 +57,27 @@
     lane = lax.broadcasted_iota(jnp.int32, (E, 128), 1)
     row = lax.broadcasted_iota(jnp.int32, (E, 128), 0)
 
-    loads = []
-    for m, ref in enumerate((gate, up, down)):
-        loads.append(pltpu.make_async_copy(ref, x.at[m], load_sem.at[m]))
-        loads[m].start()
+    barrier = pltpu.get_barrier_semaphore()
+    for d in range(N - 1):
+        to = lax.rem(me + 1 + (d + N // 3) % (N - 1), N)
+        pl.semaphore_signal(barrier, inc=1, device_id={"fsdp": to}, device_id_type=MESH)
+    for d in range(1, EP):
+        pl.semaphore_signal(barrier, inc=1, device_id={"ep": lax.rem(ep + d, EP)}, device_id_type=MESH)
+
+    def tile_at(i):
+        return pl.multiple_of(lax.rem(first + listed(TILES, i), JT) * 128, 128)
+
+    def tile_load(i):
+        part = pl.ds(tile_at(i), 128)
+        return pltpu.make_async_copy(gate.at[:, :, part], x.at[0, :, :, part], tile_sem.at[jnp.minimum(i, EARLY)])
+
+    lax.fori_loop(0, JT, lambda i, _: (tile_load(i).start(), 0)[1], 0)
+    loads = [pltpu.make_async_copy(ref, x.at[m], load_sem.at[m - 1]) for m, ref in ((1, up), (2, down))]
+    for load in loads:
+        load.start()
     rloads = [pltpu.make_async_copy(a, b, rload.at[i]) for i, (a, b) in enumerate(((rw, rw_v), (rg, rg_v)))]
     for load in rloads:
         load.start()
-
-    barrier = pltpu.get_barrier_semaphore()
-
-    def greet(d, _):
-        pl.semaphore_signal(barrier, inc=1, device_id={"fsdp": lax.rem(me + d, N)}, device_id_type=MESH)
-        return 0
-
-    def greet_ep(d, _):
-        pl.semaphore_signal(barrier, inc=1, device_id={"ep": lax.rem(ep + d, EP)}, device_id_type=MESH)
-        return 0
-
-    lax.fori_loop(1, N, greet, 0)
-    lax.fori_loop(1, EP, greet_ep, 0)
 
     def wait_bytes(ref, sem):
         pltpu.make_async_copy(ref, ref, sem).wait()
@@ -81,23 +90,24 @@
         tops[m, :, J:] = jnp.zeros((E, WIDE - J), jnp.float32)
         lax.fori_loop(0, E, one, 0)
 
+    def per_unit(top):
+        return jnp.where(top > 1e-30, LEVELS / jnp.maximum(top, 1e-30), 0.0)
+
     def scaling(m):
-        top = tops[m]
-        recip[...] = jnp.where(top > 1e-30, LEVELS / jnp.maximum(top, 1e-30), 0.0)
-
-    def listed(values, i):
-        found = 0
-        for at, value in enumerate(values):
-            found = jnp.where(i == at, value, found)
-        return found
-
-    def lay_out(m, i):
-        q = lax.rem(first + i, JT)
-        at = pl.multiple_of(q * 128, 128)
+        recip[...] = per_unit(tops[m])
+
+    def lay_out(m, at):
         for r in range(E // 2):
             v = encode(x[m, 2 * r : 2 * r + 2, :, pl.ds(at, 128)], recip[2 * r : 2 * r + 2, pl.ds(at, 128)][:, None, :])
             stage[pl.ds(r, 128, stride=E // 2), :] = v.reshape(128, 128).T
-        sent[m, pl.ds(pl.multiple_of(q * 512, 512), 512), :] = stage[...].astype(jnp.bfloat16)
+        sent[m, pl.ds(pl.multiple_of(4 * at, 512), 512), :] = stage[...].astype(jnp.bfloat16)
+
+    def first_tile(i):
+        at = tile_at(i)
+        top = jnp.max(jnp.abs(x[0, :, :, pl.ds(at, 128)]), axis=1)
+        tops[0, :, pl.ds(at, 128)] = top
+        recip[:, pl.ds(at, 128)] = per_unit(top)
+        lay_out(0, at)
 
     def rows_of(m, to):
         return sent.at[m, pl.ds(pl.multiple_of(to * ROWS, ROWS), ROWS)]
@@ -106,53 +116,51 @@
         @pl.when(to != me)
         def _():
             pltpu.make_async_remote_copy(
-                rows_of(m, to), land.at[m, me], dsend.at[m], drecv.at[m, me], device_id={"fsdp": to}, device_id_type=MESH
+                rows_of(m, to), land.at[m, me], dsend.at[m], drecv.at[m + z if m == 2 else m], device_id={"fsdp": to}, device_id_type=MESH
             ).start()
 
         @pl.when(to == me)
         def _():
             pltpu.make_async_copy(rows_of(m, to), land.at[m, me], dself.at[m]).start()
 
-    def send_tile(m, i):
-        q = lax.rem(first + i, JT)
-        to = (N * q) // JT
-
-        @pl.when(jnp.logical_or(i > 0, (JT * to) // N >= q))
-        def _():
-            send_rows(m, to)
+    def first_to(q):
+        return (N * q) // JT
+
+    def spans(q):
+        return (JT * first_to(q)) // N < q
+
+    def send_first_tile(i):
+        q = lax.rem(first + listed(TILES, i), JT)
+        to = first_to(q)
+
+        @pl.when(jnp.logical_not(spans(q)))
+        def _():
+            send_rows(0, to)
 
         for more in (1, 2):
 
-            @pl.when(to + more < (N * (q + 1)) // JT)
+            @pl.when(to + more < first_to(q + 1))
             def _():
-                send_rows(m, to + more)
-
-    def tiles(m, start, stop, make=True, send=True):
+                send_rows(0, to + more)
+
+    def send_spanning(i):
+        q = lax.rem(first + listed(TILES, i), JT)
+
+        @pl.when(spans(q))
+        def _():
+            send_rows(0, first_to(q))
+
+    def loop(start, stop, *steps):
         def one(i, _):
-            if make:
-                lay_out(m, i)
-            if send:
-                send_tile(m, i)
+            for step in steps:
+                step(i)
             return 0
 
         lax.fori_loop(start, stop, one, 0)
 
-    def send_last(m):
-        to = (N * first) // JT
-
-        @pl.when((JT * to) // N < first)
-        def _():
-            send_rows(m, to)
-
     def send_far_first(m):
-        lax.fori_loop(0, JT, lambda i, _: (lay_out(m, i), 0)[1], 0)
-
-        def one(i, _):
-            to = 4 * lax.rem(z + listed(FAR_FIRST, i // 4), 8) + lax.rem(me + i, 4)
-            send_rows(m, to)
-            return 0
-
-        lax.fori_loop(0, N, one, 0)
+        loop(0, JT, lambda i: lay_out(m, pl.multiple_of(i * 128, 128)))
+        loop(0, N, lambda i: send_rows(m, 4 * lax.rem(z + listed(FAR_FIRST, i // 4), 8) + lax.rem(me + i, 4)))
 
     own_lanes = (lane // CJ) == row
 
@@ -171,14 +179,14 @@
 
         lax.fori_loop(0, N, one, 0)
 
-    loads[0].wait()
-    maxima(0)
-    scaling(0)
-    tiles(0, 0, EARLY, send=False)
+    tops[0, :, J:] = jnp.zeros((E, WIDE - J), jnp.float32)
+    loop(0, EARLY, lambda i: tile_load(i).wait(), first_tile)
+    rest = pl.ds(0, (JT - EARLY) * 128)
+    pltpu.make_async_copy(gate.at[:, :, rest], x.at[0, :, :, rest], tile_sem.at[EARLY]).wait()
     pl.semaphore_wait(barrier, N - 1 + EP - 1)
-    tiles(0, 0, EARLY, make=False)
-    tiles(0, EARLY, JT)
-    send_last(0)
+    loop(0, EARLY, send_first_tile)
+    loop(EARLY, JT, first_tile, send_first_tile)
+    loop(0, JT, send_spanning)
 
     for load in rloads:
         load.wait()
@@ -188,8 +196,8 @@
         rhalf.at[0], rhalf.at[1], csend, crecv, device_id={"fsdp": me + 1 - 2 * core}, device_id_type=MESH
     )
     router_core.start()
+    loads[0].wait()
     loads[1].wait()
-    loads[2].wait()
     maxima(1)
     maxima(2)
     draw_lines(0)
@@ -260,6 +268,15 @@
     def line_at(m, g):
         return pl.ds((LINES * m + g) * 128, 128)
 
+    def await_last(i, plane):
+        @pl.when(jnp.logical_and(i % 2 == 0, plane == z))
+        def _():
+            wait_bytes(land.at[2, pl.ds(0, 3)], drecv.at[2 + plane])
+
+        @pl.when(jnp.logical_and(i % 2 == 0, plane != z))
+        def _():
+            wait_bytes(land.at[2, pl.ds(0, 4)], drecv.at[2 + plane])
+
     def merge(m, out):
         scale = jnp.zeros((E, 128), jnp.float32)
         for g in range(LINES):
@@ -267,6 +284,8 @@
             inv[g] = (1 / LEVELS) / jnp.where(part > 0, part, 1.0)
             scale = jnp.where(lane // CJ == g, pltpu.roll(part, CJ * g, 1), scale)
         scales[m] = scale
+        if m < 2:
+            wait_bytes(land.at[m, pl.ds(0, N - 1)], drecv.at[m])
         pltpu.make_async_copy(rows_of(m, me), land.at[m, me], dself.at[m]).wait()
         low = lane < 64
 
@@ -279,12 +298,8 @@
                 for j in range(min(CJ, JD - CJ * g)):
                     a, b = (jnp.broadcast_to(p[:, j : j + 1], (E, 128)) for p in per)
                     fac[(CJ * g + j) * E : (CJ * g + j + 1) * E, :] = jnp.where(low, a, b)
-            for side in range(2):
-
-                @pl.when(2 * c + side != me)
-                def _():
-                    wait_bytes(land.at[m, 2 * c + side], drecv.at[m, 2 * c + side])
-
+            if m == 2:
+                await_last(i, c // 2)
             a, b = (decode(land[m, 2 * c + side].astype(jnp.float32)) for side in range(2))
             v = (side_by_side(a, b) * fac[...]).astype(jnp.bfloat16)
             out[:, :, pl.ds(pl.multiple_of(c * 128, 128), 128)] = v.reshape(JD, E, 128)
@@ -358,9 +373,9 @@
             pltpu.VMEM((2, E, 128), f32),
             pltpu.VMEM((2, 8, E, 128), bf16),
         ]
-        + [dma((3,)), dma((2,))]
+        + [dma((EARLY + 1,)), dma((2,)), dma((2,))]
         + [dma] * 2
-        + [dma((3,)), dma((3, N)), dma((3,))]
+        + [dma((3,)), dma((2 + 8,)), dma((3,))]
         + [dma] * 8
         + [dma((2,))],
         compiler_params=pltpu.CompilerParams(collective_id=0, has_side_effects=True, vmem_limit_bytes=40 * 2**20),

time: 116 us -> 115 us (level)
    pallas_call x1, Pallas kernels: 113 us -> 112 us  [per_device(): pl.pallas_call(exchange, out_shape=(*(ready,) * 3, jax.ShapeDtypeStruct((...]
where the time goes in v3:
time: 115 us; the launch traced here: 114 us
  Pallas kernels  114 us (99%)
    pallas_call x1, Pallas kernels, per_device(): pl.pallas_call(exchange, out_shape=(*(ready,) * 3, jax.ShapeDtypeStruct((...  112 us

profile of v3, /device:TPU:1, one launch (start us, length us, event | category | flops | bytes accessed | tf_op | source)
XLA Modules:
  0.0 114.4 jit_solution(12705999449970663453)
XLA Ops:
  0.6 111.6 %exchange.1 = (bf16[44,8,2048]{2,1,0:T(8,128)(2,1)S(1)}, bf16[44,8,2048]{2,1,0:T(8,128)(2,1)S(1)}, bf16[44,8,2048]{2,1,0:T(8,128)(2,1)S(1)}, f32[3,8,128]{2,1,0:T(8,128)S(1)}, bf16[8,8,2,8,128]{4,3,2,1,0:T(8,128)(2,1)S(1)}) custom-call(f32[8,64,1408]{2,1,0:T(8,128)} %gate.1, f32[8,64,1408]{2,1,0:T(8,128)} %up.1, f32[8,64,1408]{2,1,0:T(8,128)} %bitcast.11, ...), custom_call_target="tpu_custom_call" | custom-call | tf_op jit(solution)/shard_map/exchange/pallas_call | solution.py:349
  112.2 2.2 %finish.1 = (bf16[44,8,2048]{2,1,0:T(8,128)(2,1)}, bf16[44,8,2048]{2,1,0:T(8,128)(2,1)}, bf16[44,8,2048]{2,1,0:T(8,128)(2,1)}, f32[8,44]{1,0:T(8,128)}, f32[8,44...) custom-call(bf16[44,8,2048]{2,1,0:T(8,128)(2,1)S(1)} %get-tuple-element.19.gate, ...), custom_call_target="tpu_custom_call" | custom-call | tf_op jit(solution)/shard_map/finish/pallas_call | solution.py:391

commit v4 on v3

--- a/solution.py
+++ b/solution.py
@@ -46,8 +46,8 @@
 
 def exchange(
     gate, up, down, rw, rg, gate_out, up_out, down_out, scales, router,
-    x, stage, sent, land, rows, tops, spread, recip, lines, got_lines, inv, fac, rw_v, rg_v, rhalf, rtile,
-    tile_sem, load_sem, rload, lsend, lrecv, dsend, drecv, dself,
+    x, stage, sent, land, rows, tops, spread, recip, others, lines, got_lines, chip_lines, got_chip_lines, inv, fac, rw_v, rg_v, rhalf, rtile,
+    tile_sem, load_sem, rload, osend, orecv, lsend, lrecv, dsend, drecv, dself,
     csend, crecv, zsend, zrecv, ysend, yrecv, esend, erecv, eself,
 ):
     me = lax.axis_index("fsdp")
@@ -168,16 +168,19 @@
         for e in range(E):
             spread[e : e + 1, :] = pltpu.roll(tops[m, e : e + 1], CJ * e, 1)
 
-        def one(to, _):
+        def one(i, _):
+            to, out = (i, lines.at[i]) if m == 0 else (2 * i + core, chip_lines.at[i])
             for g in range(LINES):
                 c0 = JD * to + CJ * g
                 at = pl.multiple_of((c0 // 128) * 128, 128)
                 near = pltpu.roll(spread[:, pl.ds(at, 256)], 256 - lax.rem(c0, 128), 1)[:, :128]
-                g0 = (LINES * m + g) * 128
-                lines[to, :, g0 : g0 + 128] = jnp.sum(jnp.where(own_lanes, near, 0.0), axis=0, keepdims=True)
+                out[:, line_at(m, g)] = jnp.sum(jnp.where(own_lanes, near, 0.0), axis=0, keepdims=True)
             return 0
 
-        lax.fori_loop(0, N, one, 0)
+        lax.fori_loop(0, N if m == 0 else N // 2, one, 0)
+
+    def line_at(m, g):
+        return pl.ds((LINES * max(m - 1, 0) + g) * 128, 128)
 
     tops[0, :, J:] = jnp.zeros((E, WIDE - J), jnp.float32)
     loop(0, EARLY, lambda i: tile_load(i).wait(), first_tile)
@@ -200,19 +203,33 @@
     loads[1].wait()
     maxima(1)
     maxima(2)
+    pair = pltpu.make_async_remote_copy(
+        tops.at[pl.ds(1, 2)], others, osend, orecv, device_id={"fsdp": me + 1 - 2 * core}, device_id_type=MESH
+    )
+    pair.start()
     draw_lines(0)
-    draw_lines(1)
-    draw_lines(2)
     got_lines[me] = lines[me]
 
-    def send_line(d, _):
+    def send_line(d):
         to = lax.rem(me + d, N)
         pltpu.make_async_remote_copy(
-            lines.at[to], got_lines.at[me], lsend, lrecv, device_id={"fsdp": to}, device_id_type=MESH
+            lines.at[to], got_lines.at[me], lsend.at[0], lrecv.at[0], device_id={"fsdp": to}, device_id_type=MESH
         ).start()
-        return 0
-
-    lax.fori_loop(1, N, send_line, 0)
+
+    def send_chip_line(d):
+        to = lax.rem(me // 2 + d, N // 2)
+        pltpu.make_async_remote_copy(
+            chip_lines.at[to], got_chip_lines.at[me // 2], lsend.at[1], lrecv.at[1],
+            device_id={"fsdp": 2 * to + core}, device_id_type=MESH,
+        ).start()
+
+    loop(1, N, send_line)
+    pair.wait()
+    for m in (1, 2):
+        tops[m] = jnp.maximum(tops[m], others[m - 1])
+        draw_lines(m)
+    got_chip_lines[me // 2] = chip_lines[me // 2]
+    loop(1, N // 2, send_chip_line)
 
     router_core.wait()
     own_side = (lane // 64) == core
@@ -237,7 +254,8 @@
         rtile.at[yh], rtile.at[yh], ysend, yrecv, device_id={"fsdp": me + 2 - 4 * yh}, device_id_type=MESH
     )
     router_y.start()
-    wait_bytes(got_lines.at[pl.ds(0, N - 1)], lrecv)
+    wait_bytes(got_lines.at[pl.ds(0, N - 1)], lrecv.at[0])
+    wait_bytes(got_chip_lines.at[pl.ds(0, N // 2 - 1)], lrecv.at[1])
     router_y.wait_recv()
 
     def router_ep(d, _):
@@ -265,9 +283,6 @@
             for_each = jnp.where(row == e, pltpu.roll(line, 128 - CJ * e, 1), for_each)
         return for_each
 
-    def line_at(m, g):
-        return pl.ds((LINES * m + g) * 128, 128)
-
     def await_last(i, plane):
         @pl.when(jnp.logical_and(i % 2 == 0, plane == z))
         def _():
@@ -280,7 +295,7 @@
     def merge(m, out):
         scale = jnp.zeros((E, 128), jnp.float32)
         for g in range(LINES):
-            part = by_expert(jnp.max(got_lines[:, :, line_at(m, g)], axis=0))
+            part = by_expert(jnp.max((got_chip_lines if m else got_lines)[:, :, line_at(m, g)], axis=0))
             inv[g] = (1 / LEVELS) / jnp.where(part > 0, part, 1.0)
             scale = jnp.where(lane // CJ == g, pltpu.roll(part, CJ * g, 1), scale)
         scales[m] = scale
@@ -292,12 +307,14 @@
         def chip(i, _):
             c = 2 * lax.rem(z + listed(ARRIVAL, i // 2), 8) + lax.rem(yh + i, 2)
             for g in range(LINES):
-                per = [
-                    by_expert(got_lines[2 * c + side, :, line_at(m, g)]) * inv[g] for side in range(2)
-                ]
+                if m == 0:
+                    got = [got_lines[2 * c + side, :, line_at(m, g)] for side in range(2)]
+                else:
+                    got = [got_chip_lines[c, :, line_at(m, g)]]
+                per = [by_expert(line) * inv[g] for line in got]
                 for j in range(min(CJ, JD - CJ * g)):
-                    a, b = (jnp.broadcast_to(p[:, j : j + 1], (E, 128)) for p in per)
-                    fac[(CJ * g + j) * E : (CJ * g + j + 1) * E, :] = jnp.where(low, a, b)
+                    both = [jnp.broadcast_to(p[:, j : j + 1], (E, 128)) for p in per]
+                    fac[(CJ * g + j) * E : (CJ * g + j + 1) * E, :] = jnp.where(low, both[0], both[-1])
             if m == 2:
                 await_last(i, c // 2)
             a, b = (decode(land[m, 2 * c + side].astype(jnp.float32)) for side in range(2))
@@ -316,7 +333,8 @@
         pltpu.make_async_copy(rtile.at[half], router.at[ep, :, half], eself.at[half]).wait()
     merge(1, up_out)
     merge(2, down_out)
-    wait_bytes(lines.at[pl.ds(0, N - 1)], lsend)
+    wait_bytes(lines.at[pl.ds(0, N - 1)], lsend.at[0])
+    wait_bytes(chip_lines.at[pl.ds(0, N // 2 - 1)], lsend.at[1])
     for m in range(3):
         wait_bytes(sent.at[m, pl.ds(0, (N - 1) * ROWS)], dsend.at[m])
 
@@ -364,8 +382,11 @@
             pltpu.VMEM((3, E, WIDE), f32),
             pltpu.VMEM((E, WIDE), f32),
             pltpu.VMEM((E, WIDE), f32),
-            pltpu.VMEM((N, 1, 3 * LINES * 128), f32),
-            pltpu.VMEM((N, 1, 3 * LINES * 128), f32),
+            pltpu.VMEM((2, E, WIDE), f32),
+            pltpu.VMEM((N, 1, LINES * 128), f32),
+            pltpu.VMEM((N, 1, LINES * 128), f32),
+            pltpu.VMEM((N // 2, 1, 2 * LINES * 128), f32),
+            pltpu.VMEM((N // 2, 1, 2 * LINES * 128), f32),
             pltpu.VMEM((LINES, E, 128), f32),
             pltpu.VMEM((JD * E, 128), f32),
             pltpu.VMEM((E, D), f32),
@@ -375,6 +396,7 @@
         ]
         + [dma((EARLY + 1,)), dma((2,)), dma((2,))]
         + [dma] * 2
+        + [dma((2,))] * 2
         + [dma((3,)), dma((2 + 8,)), dma((3,))]
         + [dma] * 8
         + [dma((2,))],

time: 115 us -> 113 us (0.983)
  Pallas kernels: 114 us -> 112 us
    pallas_call x1, Pallas kernels: 112 us -> 110 us  [per_device(): pl.pallas_call(exchange, out_shape=(*(ready,) * 3, jax.ShapeDtypeStruct((...]
where the time goes in v4:
time: 113 us
  Pallas kernels  112 us (99%)
    pallas_call x1, Pallas kernels, per_device(): pl.pallas_call(exchange, out_shape=(*(ready,) * 3, jax.ShapeDtypeStruct((...  110 us

profile of v4, /device:TPU:1, one launch (start us, length us, event | category | flops | bytes accessed | tf_op | source)
XLA Modules:
  0.0 112.9 jit_solution(5242922344072559283)
XLA Ops:
  0.6 110.1 %exchange.1 = (bf16[44,8,2048]{2,1,0:T(8,128)(2,1)S(1)}, bf16[44,8,2048]{2,1,0:T(8,128)(2,1)S(1)}, bf16[44,8,2048]{2,1,0:T(8,128)(2,1)S(1)}, f32[3,8,128]{2,1,0:T(8,128)S(1)}, bf16[8,8,2,8,128]{4,3,2,1,0:T(8,128)(2,1)S(1)}) custom-call(f32[8,64,1408]{2,1,0:T(8,128)} %gate.1, f32[8,64,1408]{2,1,0:T(8,128)} %up.1, f32[8,64,1408]{2,1,0:T(8,128)} %bitcast.11, ...), custom_call_target="tpu_custom_call" | custom-call | tf_op jit(solution)/shard_map/exchange/pallas_call | solution.py:367
  110.7 2.2 %finish.1 = (bf16[44,8,2048]{2,1,0:T(8,128)(2,1)}, bf16[44,8,2048]{2,1,0:T(8,128)(2,1)}, bf16[44,8,2048]{2,1,0:T(8,128)(2,1)}, f32[8,44]{1,0:T(8,128)}, f32[8,44...) custom-call(bf16[44,8,2048]{2,1,0:T(8,128)(2,1)S(1)} %get-tuple-element.19.gate, ...), custom_call_target="tpu_custom_call" | custom-call | tf_op jit(solution)/shard_map/finish/pallas_call | solution.py:413

commit v5 on v4

--- a/solution.py
+++ b/solution.py
@@ -283,12 +283,12 @@
             for_each = jnp.where(row == e, pltpu.roll(line, 128 - CJ * e, 1), for_each)
         return for_each
 
-    def await_last(i, plane):
-        @pl.when(jnp.logical_and(i % 2 == 0, plane == z))
+    def await_last(plane):
+        @pl.when(plane == z)
         def _():
             wait_bytes(land.at[2, pl.ds(0, 3)], drecv.at[2 + plane])
 
-        @pl.when(jnp.logical_and(i % 2 == 0, plane != z))
+        @pl.when(plane != z)
         def _():
             wait_bytes(land.at[2, pl.ds(0, 4)], drecv.at[2 + plane])
 
@@ -304,8 +304,7 @@
         pltpu.make_async_copy(rows_of(m, me), land.at[m, me], dself.at[m]).wait()
         low = lane < 64
 
-        def chip(i, _):
-            c = 2 * lax.rem(z + listed(ARRIVAL, i // 2), 8) + lax.rem(yh + i, 2)
+        def units(c, u):
             for g in range(LINES):
                 if m == 0:
                     got = [got_lines[2 * c + side, :, line_at(m, g)] for side in range(2)]
@@ -314,15 +313,22 @@
                 per = [by_expert(line) * inv[g] for line in got]
                 for j in range(min(CJ, JD - CJ * g)):
                     both = [jnp.broadcast_to(p[:, j : j + 1], (E, 128)) for p in per]
-                    fac[(CJ * g + j) * E : (CJ * g + j + 1) * E, :] = jnp.where(low, both[0], both[-1])
+                    fac[u, (CJ * g + j) * E : (CJ * g + j + 1) * E, :] = jnp.where(low, both[0], both[-1])
+
+        def plane(i, _):
+            at = lax.rem(z + listed(ARRIVAL, i), 8)
+            for u in range(2):
+                units(2 * at + u, u)
             if m == 2:
-                await_last(i, c // 2)
-            a, b = (decode(land[m, 2 * c + side].astype(jnp.float32)) for side in range(2))
-            v = (side_by_side(a, b) * fac[...]).astype(jnp.bfloat16)
-            out[:, :, pl.ds(pl.multiple_of(c * 128, 128), 128)] = v.reshape(JD, E, 128)
+                await_last(at)
+            for u in range(2):
+                c = 2 * at + u
+                a, b = (decode(land[m, 2 * c + side].astype(jnp.float32)) for side in range(2))
+                v = (side_by_side(a, b) * fac[u]).astype(jnp.bfloat16)
+                out[:, :, pl.ds(pl.multiple_of(c * 128, 128), 128)] = v.reshape(JD, E, 128)
             return 0
 
-        lax.fori_loop(0, N // 2, chip, 0)
+        lax.fori_loop(0, 8, plane, 0)
 
     merge(0, gate_out)
     wait_bytes(rtile.at[0, pl.ds(0, 7)], zsend)
@@ -388,7 +394,7 @@
             pltpu.VMEM((N // 2, 1, 2 * LINES * 128), f32),
             pltpu.VMEM((N // 2, 1, 2 * LINES * 128), f32),
             pltpu.VMEM((LINES, E, 128), f32),
-            pltpu.VMEM((JD * E, 128), f32),
+            pltpu.VMEM((2, JD * E, 128), f32),
             pltpu.VMEM((E, D), f32),
             pltpu.VMEM((1, D), f32),
             pltpu.VMEM((2, E, 128), f32),

time: 113 us -> 113 us (level)
  no operation moved by 1% of the time
where the time goes in v5:
time: 113 us
  Pallas kernels  112 us (99%)
    pallas_call x1, Pallas kernels, per_device(): pl.pallas_call(exchange, out_shape=(*(ready,) * 3, jax.ShapeDtypeStruct((...  110 us

profile of v5, /device:TPU:1, one launch (start us, length us, event | category | flops | bytes accessed | tf_op | source)
XLA Modules:
  0.0 112.6 jit_solution(2186169170123534451)
XLA Ops:
  0.6 109.7 %exchange.1 = (bf16[44,8,2048]{2,1,0:T(8,128)(2,1)S(1)}, bf16[44,8,2048]{2,1,0:T(8,128)(2,1)S(1)}, bf16[44,8,2048]{2,1,0:T(8,128)(2,1)S(1)}, f32[3,8,128]{2,1,0:T(8,128)S(1)}, bf16[8,8,2,8,128]{4,3,2,1,0:T(8,128)(2,1)S(1)}) custom-call(f32[8,64,1408]{2,1,0:T(8,128)} %gate.1, f32[8,64,1408]{2,1,0:T(8,128)} %up.1, f32[8,64,1408]{2,1,0:T(8,128)} %bitcast.11, ...), custom_call_target="tpu_custom_call" | custom-call | tf_op jit(solution)/shard_map/exchange/pallas_call | solution.py:373
  110.4 2.2 %finish.1 = (bf16[44,8,2048]{2,1,0:T(8,128)(2,1)}, bf16[44,8,2048]{2,1,0:T(8,128)(2,1)}, bf16[44,8,2048]{2,1,0:T(8,128)(2,1)}, f32[8,44]{1,0:T(8,128)}, f32[8,44...) custom-call(bf16[44,8,2048]{2,1,0:T(8,128)(2,1)S(1)} %get-tuple-element.19.gate, ...), custom_call_target="tpu_custom_call" | custom-call | tf_op jit(solution)/shard_map/finish/pallas_call | solution.py:419
